TPU v7x, 32 devices: a whole 2x2x4 slice. The times are simulated.
32 devices in a mesh: section: 2 (over x), lat: 4 (over y, core), lon: 4 (over z).
Axes of the slice: x: 2, y: 2, z: 4, core: 2. Of those that a mesh axis runs over, the one named last changes fastest.
Arguments:
- fields_in: bfloat16 [4, 96, 64, 512], P('section', None, 'lat', 'lon'), may hold values from -6 to 6
- plan: int32 [4], replicated, may hold values from 0 to 3, as said below
- in_proj: bfloat16 [64, 96], replicated, may hold values from -0.625 to 0.625
- enc_conv: bfloat16 [9, 64, 64], replicated, may hold values from -0.25 to 0.25
- down_conv: bfloat16 [9, 128, 64], replicated, may hold values from -0.25 to 0.25
- mid_conv: bfloat16 [9, 128, 128], replicated, may hold values from -0.1875 to 0.1875
- up_proj: bfloat16 [64, 128], replicated, may hold values from -0.5 to 0.5
- unite_conv: bfloat16 [9, 64, 128], replicated, may hold values from -0.1875 to 0.1875
- out_proj: bfloat16 [96, 64], replicated, may hold values from -0.75 to 0.75
Outputs:
- corrected: bfloat16 [4, 96, 64, 512], P('section', None, 'lat', 'lon')
Inputs may be any that keep to these rules, and one draw needn't show every extreme that they name: `plan`: each micro-batch appears once; the first turn takes one of the last 2 micro-batches and the last turn one of the first 2.
All inputs are finite; a program needn't handle non-finite values.
Results may differ from a plain program's by a relative error of at most 0.0072.
Values may be sent and summed in bfloat16 or wider, within the bound.
No kernel may reach another device: no remote copies, remote signals or barrier semaphores. Data moves between devices by JAX's collectives and lax.ppermute only.
A program may use at most 64 MiB of HBM per device.

v0:
```python
import jax
import jax.numpy as jnp
from jax import lax
from jax.experimental import pallas as pl
from jax.experimental.pallas import tpu as pltpu
from jax.sharding import PartitionSpec as P

BF = jnp.bfloat16
F32 = jnp.float32
HALO = 8


def gelu(x):
    inner = x * (0.7978845608028654 + 0.035677408136300125 * (x * x))
    half = 0.5 * x
    return half + half * jnp.tanh(inner)


def dot(a, b):
    return jnp.dot(a, b, preferred_element_type=F32)


def across(a, b):
    return lax.dot_general(a, b, (((0,), (0,)), ((), ())), preferred_element_type=F32)


def shift(x, by):
    n = x.shape[1]
    by = by % n
    if by == 0:
        return x
    return jnp.concatenate([x[:, by:], x[:, :by]], axis=1)


def swap_pairs(count, odd, periodic):
    pairs = []
    for low in range(1 if odd else 0, count, 2):
        high = low + 1
        if high >= count:
            if not periodic:
                continue
            high = 0
        pairs += [(low, high), (high, low)]
    return pairs


def stem_kernel(fields, w_in, stem, strip_x, strip_y, held, weights, tall, sems):
    samples, variables, height, breadth = fields.shape
    odd = lax.axis_index("lon") % 2
    first = pltpu.make_async_copy(w_in, weights, sems.at[samples])
    first.start()
    loads = [pltpu.make_async_copy(fields.at[b], held.at[b], sems.at[b]) for b in range(samples)]
    for load in loads:
        load.start()
    first.wait()
    for b in range(samples):
        loads[b].wait()
        tall[...] = held[b].astype(F32).reshape(variables * height, breadth)
        cols = [tall[pl.ds(i, variables, stride=height), :].astype(BF) for i in range(height)]
        picked = jnp.concatenate(cols, axis=1)
        full = gelu(dot(weights[...], picked)).astype(BF)
        stem[b] = full
        left = jnp.concatenate([full[:, i * breadth : i * breadth + HALO] for i in range(height)], axis=1)
        right = jnp.concatenate(
            [full[:, (i + 1) * breadth - HALO : (i + 1) * breadth] for i in range(height)], axis=1
        )
        strip_x[b] = jnp.where(odd == 1, left, right)
        strip_y[b] = jnp.where(odd == 1, right, left)


def widen_kernel(breadth, order, stem, recv_x, recv_y, half_x, half_y):
    samples = stem.shape[0]
    leaving = jnp.max(order[...])
    height = stem.shape[2] // breadth
    half = height // 2
    lon_odd = lax.axis_index("lon") % 2
    lat_odd = lax.axis_index("lat") % 2
    for b in range(samples):
        full = stem[b]
        from_x, from_y = recv_x[b], recv_y[b]
        left = jnp.where(lon_odd == 1, from_x, from_y)
        right = jnp.where(lon_odd == 1, from_y, from_x)
        halves = []
        for first in (0, half):
            pieces = []
            for m in range(4):
                for k in range(half // 4):
                    i = first + 4 * k + m
                    pieces += [
                        left[:, i * HALO : (i + 1) * HALO],
                        full[:, i * breadth : (i + 1) * breadth],
                        right[:, i * HALO : (i + 1) * HALO],
                    ]
            halves.append(jnp.concatenate(pieces, axis=1))
        slot = jnp.where(leaving == b, 0, 1)
        half_x[pl.ds(slot, 1)] = jnp.where(lat_odd == 1, halves[0], halves[1])[None]
        half_y[pl.ds(slot, 1)] = jnp.where(lat_odd == 1, halves[1], halves[0])[None]


def by_row(kernel):
    return jnp.concatenate([kernel[n] for n in range(kernel.shape[0])], axis=1)


def paired(kernel):
    flat = by_row(kernel)
    zeros = jnp.zeros((flat.shape[0], flat.shape[1] // 3), BF)
    return jnp.concatenate(
        [jnp.concatenate([flat, zeros], axis=1), jnp.concatenate([zeros, flat], axis=1)], axis=0
    )


def unet_kernel(which, lat_count, breadth, own_x, own_y, recv_x, recv_y, enc, down, mid, w_up, unite, *refs):
    if which == 1:
        w_out, merged, w_out_held = refs[:3]
        w_out_held[...] = w_out[...]
    else:
        merged = refs[0]
    quads, zz1, zz2, zz3, zz4 = refs[1 + 2 * which :]
    pitch = breadth + 2 * HALO
    lat = lax.axis_index("lat")
    even = lat % 2 == 0
    mine_x, mine_y, far_x, far_y = own_x[which], own_y[which], recv_x[which], recv_y[which]
    quads[0] = jnp.where(even, far_y, far_x)
    quads[1] = jnp.where(even, mine_y, mine_x)
    quads[2] = jnp.where(even, mine_x, mine_y)
    quads[3] = jnp.where(even, far_x, far_y)
    c0 = quads.shape[1]
    lanes = quads.shape[2]
    quarter = lanes // 4
    low_edge = lat == 0
    high_edge = lat == lat_count - 1

    def keep(width, low, high):
        lane = lax.broadcasted_iota(jnp.int32, (1, width), 1)
        drop = (low_edge & (lane < low)) | (high_edge & (lane >= high))
        return jnp.where(drop, 0.0, 1.0).astype(F32)

    full_keep = keep(lanes, quarter, lanes - quarter)
    planes = [
        jnp.concatenate([quads[s, :, m * quarter : (m + 1) * quarter] for s in range(4)], axis=1)
        for m in range(4)
    ]
    rows = [shift(planes[3], -pitch)] + planes + [shift(planes[0], pitch)]
    for j, row in enumerate(rows):
        base = j * 3 * c0
        zz1[base : base + c0] = shift(row, -1)
        zz1[base + c0 : base + 2 * c0] = row
        zz1[base + 2 * c0 : base + 3 * c0] = shift(row, 1)
    skip = []
    for q in range(2):
        out = dot(paired(enc), zz1[2 * q * 3 * c0 : (2 * q + 4) * 3 * c0])
        out = (gelu(out) * full_keep).astype(BF)
        skip += [out[:c0], out[c0:]]

    blocks = -(-lanes // 256)
    spare = blocks * 256 - lanes
    to_lane = lax.broadcasted_iota(jnp.int32, (512, 128), 1)
    from_lane = lax.broadcasted_iota(jnp.int32, (512, 128), 0) % 256
    gather = jnp.where(from_lane // 2 == to_lane, 0.25, 0.0).astype(BF)
    stacked = []
    for h in range(2):
        pair = [
            jnp.concatenate([skip[2 * h + e], jnp.zeros((c0, spare), BF)], axis=1) if spare else skip[2 * h + e]
            for e in range(2)
        ]
        for t in range(blocks):
            stacked.append(
                jnp.concatenate([pair[0][:, 256 * t : 256 * (t + 1)], pair[1][:, 256 * t : 256 * (t + 1)]], axis=1)
            )
    small = dot(jnp.concatenate(stacked, axis=0), gather).astype(BF)
    pooled = [
        jnp.concatenate([small[(h * blocks + t) * c0 : (h * blocks + t + 1) * c0] for t in range(blocks)], axis=1)
        for h in range(2)
    ]
    half_lanes = 128 * blocks
    half_pitch = pitch // 2
    half_keep = keep(half_lanes, quarter // 2, (lanes - quarter) // 2)

    def halves(scratch, source):
        width = source[0].shape[0]
        for j, row in enumerate(
            (shift(source[1], -half_pitch), source[0], source[1], shift(source[0], half_pitch))
        ):
            base = j * 3 * width
            scratch[base : base + width] = shift(row, -1)
            scratch[base + width : base + 2 * width] = row
            scratch[base + 2 * width : base + 3 * width] = shift(row, 1)

    halves(zz2, pooled)
    w_down = jnp.concatenate([down[n] for n in range(down.shape[0])], axis=0)
    deep = []
    for h in range(2):
        out = across(w_down, zz2[h * 3 * c0 : (h + 3) * 3 * c0])
        deep.append((gelu(out) * half_keep).astype(BF))
    halves(zz3, deep)
    c1 = deep[0].shape[0]
    lifted = []
    for h in range(2):
        out = dot(by_row(mid), zz3[h * 3 * c1 : (h + 3) * 3 * c1])
        middle = (gelu(out) + deep[h].astype(F32)).astype(BF)
        lifted.append((dot(w_up[...], middle) * half_keep).astype(BF))
    wide_lane = lax.broadcasted_iota(jnp.int32, (128, 256), 1)
    thin_lane = lax.broadcasted_iota(jnp.int32, (128, 256), 0)
    spread = jnp.where(wide_lane // 2 == thin_lane, 1.0, 0.0).astype(BF)
    stacked = jnp.concatenate(
        [lifted[h][:, 128 * t : 128 * (t + 1)] for h in range(2) for t in range(blocks)], axis=0
    )
    large = dot(stacked, spread).astype(BF)
    raised = [
        jnp.concatenate([large[(h * blocks + t) * c0 : (h * blocks + t + 1) * c0] for t in range(blocks)], axis=1)
        for h in range(2)
    ]
    start = quarter // 128 * 128
    span = zz4.shape[1]
    lift_rows = [(raised[1], -pitch), (raised[0], 0), (raised[0], 0), (raised[1], 0), (raised[1], 0), (raised[0], pitch)]
    skip_rows = [(skip[3], -pitch)] + [(s, 0) for s in skip] + [(skip[0], pitch)]
    for j in range(6):
        for b in range(3):
            base = (3 * j + b) * 2 * c0
            row, move = lift_rows[j]
            at = start + move + b - 1
            zz4[base : base + c0] = row[:, at : at + span]
            row, move = skip_rows[j]
            zz4[base + c0 : base + 2 * c0] = row[:, at : at + span]
    joined = []
    for q in range(2):
        out = dot(paired(unite), zz4[2 * q * 6 * c0 : (2 * q + 4) * 6 * c0])
        out = gelu(out).astype(BF)
        joined += [out[:c0], out[c0:]]
    rest = quarter - start
    pieces = []
    for k in range(lanes // pitch // 2):
        for m in range(4):
            at = rest + k * pitch + HALO
            pieces.append(joined[m][:, at : at + breadth])
    merged[...] = jnp.concatenate(pieces, axis=1)


def project_kernel(map_a, map_b, w_out, out, tall, ready, sems):
    section = lax.axis_index("section")
    variables, height, breadth = out.shape[1:]
    stores = []
    for n, source in enumerate((map_b, map_a)):
        full = across(w_out[...], source[...])
        for i in range(height):
            tall[n, pl.ds(i, variables, stride=height), :] = full[:, i * breadth : (i + 1) * breadth]
        ready[n] = tall[n].astype(BF).reshape(variables, height, breadth)
        store = pltpu.make_async_copy(ready.at[n], out.at[section if n == 1 else 1 - section], sems.at[n])
        store.start()
        stores.append(store)
    for store in stores:
        store.wait()


def call(kernel, outs, scratch, args, mebibytes, spaces=None, out_space=None):
    vmem = pl.BlockSpec(memory_space=pltpu.VMEM)
    return pl.pallas_call(
        kernel,
        out_shape=outs,
        in_specs=spaces if spaces else [vmem] * len(args),
        out_specs=out_space or jax.tree.map(lambda _: vmem, outs),
        scratch_shapes=scratch,
        compiler_params=pltpu.CompilerParams(vmem_limit_bytes=int(mebibytes * 2**20)),
    )(*args)


def shards(fields_in, plan, in_proj, enc_conv, down_conv, mid_conv, up_proj, unite_conv, out_proj):
    samples, variables, height, breadth = fields_in.shape
    c0, c1 = in_proj.shape[0], up_proj.shape[1]
    sections, lats, lons = lax.axis_size("section"), lax.axis_size("lat"), lax.axis_size("lon")
    shape = jax.ShapeDtypeStruct
    lanes = height // 2 * (breadth + 2 * HALO)

    hbm, vmem, smem = (pl.BlockSpec(memory_space=s) for s in (pltpu.HBM, pltpu.VMEM, pltpu.SMEM))
    strip = shape((samples, c0, height * HALO), BF)
    stem, strip_x, strip_y = call(
        stem_kernel,
        (shape((samples, c0, height * breadth), BF), strip, strip),
        [
            pltpu.VMEM((samples, variables, height, breadth), BF),
            pltpu.VMEM((c0, variables), BF),
            pltpu.VMEM((variables * height, breadth), F32),
            pltpu.SemaphoreType.DMA((samples + 1,)),
        ],
        (fields_in, in_proj),
        53,
        [hbm, hbm],
    )
    recv_y = lax.ppermute(strip_y, "lon", swap_pairs(lons, True, True))
    recv_x = lax.ppermute(strip_x, "lon", swap_pairs(lons, False, True))
    half = shape((samples, c0, lanes), BF)
    leaving = jnp.where(lax.axis_index("section") == 0, plan[2 * samples - 1], plan[0] - samples)
    order = jnp.broadcast_to(leaving.astype(F32), (8, 128))
    crossing = (plan[samples - 1] >= samples).astype(jnp.int32)
    recv_x, recv_y, order, crossing = lax.optimization_barrier((recv_x, recv_y, order, crossing))
    half_x, half_y = call(
        lambda *refs: widen_kernel(breadth, *refs), (half, half), [], (order, stem, recv_x, recv_y), 8
    )
    far_y = lax.ppermute(half_y, "lat", swap_pairs(lats, True, False))
    far_x = lax.ppermute(half_x, "lat", swap_pairs(lats, False, False))
    half_lanes = -(-lanes // 256) * 128
    span = -(-(3 * (lanes // 4)) // 128) * 128 - lanes // 4 // 128 * 128

    def unet(which):
        return call(
            lambda *refs: unet_kernel(which, lats, breadth, *refs),
            (shape((c0, height * breadth), BF), shape((c0, variables), BF))[: 1 + which],
            [
                pltpu.VMEM((4, c0, lanes), BF),
                pltpu.VMEM((6 * 3 * c0, lanes), BF),
                pltpu.VMEM((4 * 3 * c0, half_lanes), BF),
                pltpu.VMEM((4 * 3 * c1, half_lanes), BF),
                pltpu.VMEM((6 * 6 * c0, span), BF),
            ],
            (half_x, half_y, far_x, far_y, enc_conv, down_conv.transpose(0, 2, 1), mid_conv)
            + (up_proj, unite_conv, out_proj.T)[: 2 + which],
            20,
            [vmem] * (9 + which),
        )

    swap = [(0, 1), (1, 0)]
    map_a = lax.ppermute(unet(0)[0], "section", swap)
    map_b, w_out = unet(1)
    map_b = lax.cond(
        crossing > 0, lambda v: lax.ppermute(v, "section", swap), lambda v: v, map_b
    )
    return call(
        project_kernel,
        shape((samples, variables, height, breadth), BF),
        [
            pltpu.VMEM((2, variables * height, breadth), F32),
            pltpu.VMEM((2, variables, height, breadth), BF),
            pltpu.SemaphoreType.DMA((2,)),
        ],
        (map_a, map_b, w_out),
        12,
        out_space=hbm,
    )


def solution(mesh):
    return jax.shard_map(
        shards,
        mesh=mesh,
        in_specs=(P("section", None, "lat", "lon"), P(), P(), P(), P(), P(), P(), P(), P()),
        out_specs=P("section", None, "lat", "lon"),
        check_vma=False,
    )
```

profile of v0, /device:TPU:1, one launch (start us, length us, event | category | flops | bytes accessed | tf_op | source)
XLA Modules:
  0.0 37.7 jit_solution(1397006620957741470)
XLA Ops:
  0.0 0.0 copy-start.6
  0.0 0.7 %copy-done.6 = bf16[64,96]{1,0:T(8,128)(2,1)S(1)} copy-done((bf16[64,96]{1,0:T(8,128)(2,1)S(1)}, bf16[64,96]{1,0:T(8,128)(2,1)}, u32[]{:S(2)}) %copy-start.6) | copy-done | bytes 12312
  0.7 0.0 copy-start.3
  0.7 2.2 %shard_map.91 = (bf16[2,64,2048]{2,1,0:T(8,128)(2,1)S(1)}, bf16[2,64,128]{2,1,0:T(8,128)(2,1)S(1)}, bf16[2,64,128]{2,1,0:T(8,128)(2,1)S(1)}) custom-call(bf16[2,96,16,128]{3,2,1,0:T(8,128)(2,1)} %fields.1, bf16[64,96]{1,0:T(8,128)(2,1)S(1)} %copy-done.6), custom_call_target="tpu_custom_call" | custom-call | tf_op jit(solution)/shard_map/pallas_call | solution.py:257
  2.9 0.0 copy-start.7
  2.9 2.2 %collective-permute-start.1 = (bf16[2,64,128]{2,1,0:T(8,128)(2,1)S(1)}, bf16[2,64,128]{2,1,0:T(8,128)(2,1)S(1)}, u32[]{:S(2)}, u32[]{:S(2)}) collective-permute-start(bf16[2,64,128]{2,1,0:T(8,128)(2,1)S(1)} %get-tuple-element.21), channel_id=1, source_target_pairs={{0,1},{1,0},{2,3},{3,2},{4,5},{5,4},{6,7},{7,6},{8,9},{9,8},{10,11... | collective-permute-start | bytes 98312 | tf_op jit(solution)/shard_map/ppermute | solution.py:290
  5.1 2.2 %collective-permute-start.2 = (bf16[2,64,128]{2,1,0:T(8,128)(2,1)S(1)}, bf16[2,64,128]{2,1,0:T(8,128)(2,1)S(1)}, u32[]{:S(2)}, u32[]{:S(2)}) collective-permute-start(bf16[2,64,128]{2,1,0:T(8,128)(2,1)S(1)} %get-tuple-element.22), channel_id=1, source_target_pairs={{1,2},{2,1},{3,0},{0,3},{5,6},{6,5},{7,4},{4,7},{9,10},{10,9},{11,... | collective-permute-start | bytes 98312 | tf_op jit(solution)/shard_map/ppermute | solution.py:289
  7.3 0.0 copy-done.7
  7.3 0.7 %fusion = (s32[1]{0:T(128)}, s32[1]{0:T(128)}, s32[1]{0:T(128)}) fusion(s32[4]{0:T(128)S(1)} %copy-done.7), kind=kLoop, calls=%fused_computation | loop fusion | bytes 24 | tf_op jit(solution)/shard_map/slice | solution.py:294
  9.4 0.0 copy-start.4
  10.0 0.0 collective-permute-done.1.refs_2_
  10.1 0.0 collective-permute-done.2.refs_3_
  10.1 0.0 copy-start
  10.1 0.0 copy-start.1
  10.1 0.0 copy-start.2
  10.1 0.4 %shard_map.92 = (bf16[2,64,1152]{2,1,0:T(8,128)(2,1)S(1)}, bf16[2,64,1152]{2,1,0:T(8,128)(2,1)S(1)}) custom-call(f32[8,128]{1,0:T(8,128)S(1)} %broadcast_in_dim.3.refs_0_, bf16[2,64,2048]{2,1,0:T(8,128)(2,1)S(1)} %get-tuple-element.24.refs_1_, bf16[2,64,128]{2,1,0:T(8,128)(2,1)S(1)} %collective-permute-done.1.refs_2_, ...), custom_call_target="tpu_custom_call" | custom-call | tf_op jit(solution)/shard_map/pallas_call | solution.py:257
  10.5 1.8 %collective-permute-start.3 = (bf16[2,64,1152]{2,1,0:T(8,128)(2,1)S(1)}, bf16[2,64,1152]{2,1,0:T(8,128)(2,1)S(1)}, u32[]{:S(2)}, u32[]{:S(2)}) collective-permute-start(bf16[2,64,1152]{2,1,0:T(8,128)(2,1)S(1)} %get-tuple-element.27.refs_0_), channel_id=1, source_target_pairs={{0,4},{4,0},{8,12},{12,8},{1,5},{5,1},{9,13},{13,9},{2,6},{6,2},{1... | collective-permute-start | bytes 884744 | tf_op jit(solution)/shard_map/ppermute | solution.py:300
  12.3 3.0 %collective-permute-start.4 = (bf16[2,64,1152]{2,1,0:T(8,128)(2,1)S(1)}, bf16[2,64,1152]{2,1,0:T(8,128)(2,1)S(1)}, u32[]{:S(2)}, u32[]{:S(2)}) collective-permute-start(bf16[2,64,1152]{2,1,0:T(8,128)(2,1)S(1)} %get-tuple-element.28.refs_1_), channel_id=1, source_target_pairs={{4,8},{8,4},{5,9},{9,5},{6,10},{10,6},{7,11},{11,7},{20,24},{24,20... | collective-permute-start | bytes 884744 | tf_op jit(solution)/shard_map/ppermute | solution.py:299
  15.3 0.0 collective-permute-done.3.refs_2_
  15.4 5.0 %collective-permute-done.4.refs_3_ = bf16[2,64,1152]{2,1,0:T(8,128)(2,1)S(1)} collective-permute-done((bf16[2,64,1152]{2,1,0:T(8,128)(2,1)S(1)}, bf16[2,64,1152]{2,1,0:T(8,128)(2,1)S(1)}, u32[]{:S(2)}, u32[]{:S(2)}) %collective-permute-start.4) | collective-permute-done | bytes 294944 | tf_op jit(solution)/shard_map/ppermute | solution.py:299
  20.3 0.0 copy-done.3
  20.3 0.0 copy-done.4
  20.3 0.0 copy-done
  20.3 0.0 copy-done.1
  20.3 0.0 copy-done.2
  20.3 0.0 copy-start.5
  20.4 4.6 %shard_map.93 = bf16[64,2048]{1,0:T(8,128)(2,1)S(1)} custom-call(bf16[2,64,1152]{2,1,0:T(8,128)(2,1)S(1)} %get-tuple-element.27.refs_0_, bf16[2,64,1152]{2,1,0:T(8,128)(2,1)S(1)} %get-tuple-element.28.refs_1_, bf16[2,64,1152]{2,1,0:T(8,128)(2,1)S(1)} %collective-permute-done.3.refs_2_, bf16[2,64,1152]{2,1,0:T(8,128)(2,1)S(1)} %collective-permute-done.4.refs_3_, ...), custom_call_target="tpu_custom_call" | custom-call | tf_op jit(solution)/shard_map/pallas_call | solution.py:257
  25.0 1.3 %collective-permute-start.5 = (bf16[64,2048]{1,0:T(8,128)(2,1)S(1)}, bf16[64,2048]{1,0:T(8,128)(2,1)S(1)}, u32[]{:S(2)}, u32[]{:S(2)}) collective-permute-start(bf16[64,2048]{1,0:T(8,128)(2,1)S(1)} %shard_map.93), channel_id=1, source_target_pairs={{0,16},{16,0},{1,17},{17,1},{2,18},{18,2},{3,19},{19,3},{4,20},{20... | collective-permute-start | bytes 786440 | tf_op jit(solution)/shard_map/ppermute | solution.py:322
  26.2 0.0 copy-done.5
  26.2 4.6 %shard_map.94 = (bf16[64,2048]{1,0:T(8,128)(2,1)S(1)}, bf16[64,96]{1,0:T(8,128)(2,1)S(1)}) custom-call(bf16[2,64,1152]{2,1,0:T(8,128)(2,1)S(1)} %get-tuple-element.27.refs_0_, bf16[2,64,1152]{2,1,0:T(8,128)(2,1)S(1)} %get-tuple-element.28.refs_1_, bf16[2,64,1152]{2,1,0:T(8,128)(2,1)S(1)} %collective-permute-done.3.refs_2_, ...), custom_call_target="tpu_custom_call" | custom-call | tf_op jit(solution)/shard_map/pallas_call | solution.py:257
  30.9 5.3 %conditional.1 = (bf16[64,2048]{1,0:T(8,128)(2,1)S(1)}) conditional(s32[]{:T(128)} %convert_element_type.15, bf16[64,2048]{1,0:T(8,128)(2,1)S(1)} %get-tuple-element.30, bf16[64,2048]{1,0:T(8,128)(2,1)S(1)} %get-tuple-element.30), branch_computations={%region_0.1_spmd, %region_1.2_spmd} | conditional | bytes 1572912 | solution.py:324
  30.9 0.3 collective-permute-start
  31.2 5.0 %collective-permute-done = bf16[64,2048]{1,0:T(8,128)(2,1)S(1)} collective-permute-done((bf16[64,2048]{1,0:T(8,128)(2,1)S(1)}, bf16[64,2048]{1,0:T(8,128)(2,1)S(1)}, u32[]{:S(2)}, u32[]{:S(2)}) %collective-permute-start) | collective-permute-done | bytes 262176 | tf_op jit(solution)/shard_map/cond/branch_1_fun/ppermute | solution.py:325
  36.2 0.0 collective-permute-done.5.map_a
  36.2 1.5 %shard_map.95 = bf16[2,96,16,128]{3,2,1,0:T(8,128)(2,1)} custom-call(bf16[64,2048]{1,0:T(8,128)(2,1)S(1)} %collective-permute-done.5.map_a, bf16[64,2048]{1,0:T(8,128)(2,1)S(1)} %get-tuple-element.35.map_b, bf16[64,96]{1,0:T(8,128)(2,1)S(1)} %get-tuple-element.31.w_out), custom_call_target="tpu_custom_call" | custom-call | tf_op jit(solution)/shard_map/pallas_call | solution.py:257
  (2 shorter events, 0.0 us)
Async XLA Ops:
  0.0 0.7 %copy-start.6 = (bf16[64,96]{1,0:T(8,128)(2,1)S(1)}, bf16[64,96]{1,0:T(8,128)(2,1)}, u32[]{:S(2)}) copy-start(bf16[64,96]{1,0:T(8,128)(2,1)} %w_in.1) | copy-start | bytes 36868
  0.7 19.6 %copy-start.3 = (bf16[9,64,128]{2,1,0:T(8,128)(2,1)S(1)}, bf16[9,64,128]{2,1,0:T(8,128)(2,1)}, u32[]{:S(2)}) copy-start(bf16[9,64,128]{2,1,0:T(8,128)(2,1)} %refs_8_.3) | copy-start | bytes 442372
  2.9 4.4 %copy-start.7 = (s32[4]{0:T(128)S(1)}, s32[4]{0:T(128)}, u32[]{:S(2)}) copy-start(s32[4]{0:T(128)} %param.12) | copy-start | bytes 52
  2.9 7.1 %collective-permute-start.1 = (bf16[2,64,128]{2,1,0:T(8,128)(2,1)S(1)}, bf16[2,64,128]{2,1,0:T(8,128)(2,1)S(1)}, u32[]{:S(2)}, u32[]{:S(2)}) collective-permute-start(bf16[2,64,128]{2,1,0:T(8,128)(2,1)S(1)} %get-tuple-element.21), channel_id=1, source_target_pairs={{0,1},{1,0},{2,3},{3,2},{4,5},{5,4},{6,7},{7,6},{8,9},{9,8},{10,11... | collective-permute-start | bytes 98312 | tf_op jit(solution)/shard_map/ppermute | solution.py:290
  5.1 4.9 %collective-permute-start.2 = (bf16[2,64,128]{2,1,0:T(8,128)(2,1)S(1)}, bf16[2,64,128]{2,1,0:T(8,128)(2,1)S(1)}, u32[]{:S(2)}, u32[]{:S(2)}) collective-permute-start(bf16[2,64,128]{2,1,0:T(8,128)(2,1)S(1)} %get-tuple-element.22), channel_id=1, source_target_pairs={{1,2},{2,1},{3,0},{0,3},{5,6},{6,5},{7,4},{4,7},{9,10},{10,9},{11,... | collective-permute-start | bytes 98312 | tf_op jit(solution)/shard_map/ppermute | solution.py:289
  9.4 11.0 %copy-start.4 = (bf16[64,128]{1,0:T(8,128)(2,1)S(1)}, bf16[64,128]{1,0:T(8,128)(2,1)}, u32[]{:S(2)}) copy-start(bf16[64,128]{1,0:T(8,128)(2,1)} %refs_7_.3) | copy-start | bytes 49156
  10.1 10.3 %copy-start = (bf16[9,128,128]{2,1,0:T(8,128)(2,1)S(1)}, bf16[9,128,128]{2,1,0:T(8,128)(2,1)}, u32[]{:S(2)}) copy-start(bf16[9,128,128]{2,1,0:T(8,128)(2,1)} %refs_6_.3) | copy-start | bytes 884740
  10.1 10.2 %copy-start.1 = (bf16[9,64,64]{2,1,0:T(8,128)(2,1)S(1)}, bf16[9,64,64]{2,1,0:T(8,128)(2,1)}, u32[]{:S(2)}) copy-start(bf16[9,64,64]{2,1,0:T(8,128)(2,1)} %refs_4_.3) | copy-start | bytes 221188
  10.1 10.2 %copy-start.2 = (bf16[9,128,64]{1,2,0:T(8,128)(2,1)S(1)}, bf16[9,128,64]{1,2,0:T(8,128)(2,1)}, u32[]{:S(2)}) copy-start(bf16[9,128,64]{1,2,0:T(8,128)(2,1)} %param.15) | copy-start | bytes 442372
  10.5 4.8 %collective-permute-start.3 = (bf16[2,64,1152]{2,1,0:T(8,128)(2,1)S(1)}, bf16[2,64,1152]{2,1,0:T(8,128)(2,1)S(1)}, u32[]{:S(2)}, u32[]{:S(2)}) collective-permute-start(bf16[2,64,1152]{2,1,0:T(8,128)(2,1)S(1)} %get-tuple-element.27.refs_0_), channel_id=1, source_target_pairs={{0,4},{4,0},{8,12},{12,8},{1,5},{5,1},{9,13},{13,9},{2,6},{6,2},{1... | collective-permute-start | bytes 884744 | tf_op jit(solution)/shard_map/ppermute | solution.py:300
  12.3 8.0 %collective-permute-start.4 = (bf16[2,64,1152]{2,1,0:T(8,128)(2,1)S(1)}, bf16[2,64,1152]{2,1,0:T(8,128)(2,1)S(1)}, u32[]{:S(2)}, u32[]{:S(2)}) collective-permute-start(bf16[2,64,1152]{2,1,0:T(8,128)(2,1)S(1)} %get-tuple-element.28.refs_1_), channel_id=1, source_target_pairs={{4,8},{8,4},{5,9},{9,5},{6,10},{10,6},{7,11},{11,7},{20,24},{24,20... | collective-permute-start | bytes 884744 | tf_op jit(solution)/shard_map/ppermute | solution.py:299
  20.3 5.9 %copy-start.5 = (bf16[96,64]{0,1:T(8,128)(2,1)S(1)}, bf16[96,64]{0,1:T(8,128)(2,1)}, u32[]{:S(2)}) copy-start(bf16[96,64]{0,1:T(8,128)(2,1)} %param.19) | copy-start | bytes 36868
  25.0 11.2 %collective-permute-start.5 = (bf16[64,2048]{1,0:T(8,128)(2,1)S(1)}, bf16[64,2048]{1,0:T(8,128)(2,1)S(1)}, u32[]{:S(2)}, u32[]{:S(2)}) collective-permute-start(bf16[64,2048]{1,0:T(8,128)(2,1)S(1)} %shard_map.93), channel_id=1, source_target_pairs={{0,16},{16,0},{1,17},{17,1},{2,18},{18,2},{3,19},{19,3},{4,20},{20... | collective-permute-start | bytes 786440 | tf_op jit(solution)/shard_map/ppermute | solution.py:322
  30.9 5.3 %collective-permute-start = (bf16[64,2048]{1,0:T(8,128)(2,1)S(1)}, bf16[64,2048]{1,0:T(8,128)(2,1)S(1)}, u32[]{:S(2)}, u32[]{:S(2)}) collective-permute-start(bf16[64,2048]{1,0:T(8,128)(2,1)S(1)} %param.1), channel_id=1, source_target_pairs={{0,16},{16,0},{1,17},{17,1},{2,18},{18,2},{3,19},{19,3},{4,20},{20... | collective-permute-start | bytes 786440 | tf_op jit(solution)/shard_map/cond/branch_1_fun/ppermute | solution.py:325
where the time goes:
time: 37.9 us; the launch traced here: 37.7 us
  Pallas kernels  13.3 us (35%)
  starting transfers between devices  10.8 us (28%)
  waiting for transfers between devices  9.94 us (26%)
  between operations  2.19 us (6%)
  local copies, waits for them, and re-layouts  1.44 us (4%)
    pallas_call x5, Pallas kernels, call(): pl.pallas_call(kernel, out_shape=outs, in_specs=spaces if spaces else [vm...  13.3 us
    ppermute x1, waiting for transfers between devices, shards(): lax.ppermute(v, 'section', swap)  4.97 us
    ppermute x1, waiting for transfers between devices, shards(): far_y = lax.ppermute(half_y, 'lat', swap_pairs(lats, True, False))  4.97 us
    ppermute x1, starting transfers between devices, shards(): far_y = lax.ppermute(half_y, 'lat', swap_pairs(lats, True, False))  3.05 us
    ppermute x1, starting transfers between devices, shards(): recv_y = lax.ppermute(strip_y, 'lon', swap_pairs(lons, True, True))  2.2 us
    ppermute x1, starting transfers between devices, shards(): recv_x = lax.ppermute(strip_x, 'lon', swap_pairs(lons, False, True))  2.18 us
    ppermute x1, starting transfers between devices, shards(): far_x = lax.ppermute(half_x, 'lat', swap_pairs(lats, False, False))  1.76 us
    ppermute x1, starting transfers between devices, shards(): map_a = lax.ppermute(unet(0)[0], 'section', swap)  1.27 us
  transfers between devices with their start and end apart: 6, of which 2 were waited for; matrix products, arithmetic and copies ran while one was open for 2% of the time, Pallas kernels for 12%

commit v1 on v0

--- a/solution.py
+++ b/solution.py
@@ -8,6 +8,7 @@
 BF = jnp.bfloat16
 F32 = jnp.float32
 HALO = 8
+LIMIT_ROWS = 52.7
 
 
 def gelu(x):
@@ -44,21 +45,23 @@
     return pairs
 
 
-def stem_kernel(fields, w_in, stem, strip_x, strip_y, held, weights, tall, sems):
+def rows_kernel(fields, picked, held, tall, sems):
     samples, variables, height, breadth = fields.shape
-    odd = lax.axis_index("lon") % 2
-    first = pltpu.make_async_copy(w_in, weights, sems.at[samples])
-    first.start()
     loads = [pltpu.make_async_copy(fields.at[b], held.at[b], sems.at[b]) for b in range(samples)]
     for load in loads:
         load.start()
-    first.wait()
     for b in range(samples):
         loads[b].wait()
         tall[...] = held[b].astype(F32).reshape(variables * height, breadth)
-        cols = [tall[pl.ds(i, variables, stride=height), :].astype(BF) for i in range(height)]
-        picked = jnp.concatenate(cols, axis=1)
-        full = gelu(dot(weights[...], picked)).astype(BF)
+        for i in range(height):
+            picked[b, :, i * breadth : (i + 1) * breadth] = tall[pl.ds(i, variables, stride=height), :].astype(BF)
+
+
+def stem_kernel(height, breadth, picked, w_in, stem, strip_x, strip_y):
+    samples = picked.shape[0]
+    odd = lax.axis_index("lon") % 2
+    for b in range(samples):
+        full = gelu(dot(w_in[...], picked[b])).astype(BF)
         stem[b] = full
         left = jnp.concatenate([full[:, i * breadth : i * breadth + HALO] for i in range(height)], axis=1)
         right = jnp.concatenate(
@@ -68,9 +71,12 @@
         strip_y[b] = jnp.where(odd == 1, right, left)
 
 
-def widen_kernel(breadth, order, stem, recv_x, recv_y, half_x, half_y):
+def widen_kernel(breadth, plan, stem, recv_x, recv_y, half_x, half_y):
     samples = stem.shape[0]
-    leaving = jnp.max(order[...])
+    turns = plan[...].astype(F32).reshape(1, 2 * samples)
+    turn = lax.broadcasted_iota(jnp.int32, turns.shape, 1)
+    first, last = (jnp.sum(jnp.where(turn == n, turns, 0.0)) for n in (0, 2 * samples - 1))
+    leaving = jnp.where(lax.axis_index("section") == 0, last, first - samples)
     height = stem.shape[2] // breadth
     half = height // 2
     lon_odd = lax.axis_index("lon") % 2
@@ -273,28 +279,32 @@
 
     hbm, vmem, smem = (pl.BlockSpec(memory_space=s) for s in (pltpu.HBM, pltpu.VMEM, pltpu.SMEM))
     strip = shape((samples, c0, height * HALO), BF)
-    stem, strip_x, strip_y = call(
-        stem_kernel,
-        (shape((samples, c0, height * breadth), BF), strip, strip),
+    picked = call(
+        rows_kernel,
+        shape((samples, variables, height * breadth), BF),
         [
             pltpu.VMEM((samples, variables, height, breadth), BF),
-            pltpu.VMEM((c0, variables), BF),
             pltpu.VMEM((variables * height, breadth), F32),
-            pltpu.SemaphoreType.DMA((samples + 1,)),
+            pltpu.SemaphoreType.DMA((samples,)),
         ],
-        (fields_in, in_proj),
-        53,
-        [hbm, hbm],
+        (fields_in,),
+        LIMIT_ROWS,
+        [hbm],
+    )
+    stem, strip_x, strip_y = call(
+        lambda *refs: stem_kernel(height, breadth, *refs),
+        (shape((samples, c0, height * breadth), BF), strip, strip),
+        [],
+        (picked, in_proj),
+        12,
     )
     recv_y = lax.ppermute(strip_y, "lon", swap_pairs(lons, True, True))
     recv_x = lax.ppermute(strip_x, "lon", swap_pairs(lons, False, True))
     half = shape((samples, c0, lanes), BF)
-    leaving = jnp.where(lax.axis_index("section") == 0, plan[2 * samples - 1], plan[0] - samples)
-    order = jnp.broadcast_to(leaving.astype(F32), (8, 128))
     crossing = (plan[samples - 1] >= samples).astype(jnp.int32)
-    recv_x, recv_y, order, crossing = lax.optimization_barrier((recv_x, recv_y, order, crossing))
+    recv_x, recv_y, crossing = lax.optimization_barrier((recv_x, recv_y, crossing))
     half_x, half_y = call(
-        lambda *refs: widen_kernel(breadth, *refs), (half, half), [], (order, stem, recv_x, recv_y), 8
+        lambda *refs: widen_kernel(breadth, *refs), (half, half), [], (plan, stem, recv_x, recv_y), 8
     )
     far_y = lax.ppermute(half_y, "lat", swap_pairs(lats, True, False))
     far_x = lax.ppermute(half_x, "lat", swap_pairs(lats, False, False))

time: 37.9 us -> 37.2 us (0.982)
  between operations: 2.19 us -> 0.78 us
  waiting for transfers between devices: 9.94 us -> 11.3 us
  local copies, waits for them, and re-layouts: 1.44 us -> 0.64 us
    ppermute x1, waiting for transfers between devices: 0.01 us -> 1.4 us  [shards(): recv_y = lax.ppermute(strip_y, 'lon', swap_pairs(lons, True, True))]
    unnamed x16, local copies, waits for them, and re-layouts: 0.76 us -> 0.04 us
    pallas_call x5 -> x6, Pallas kernels: 13.3 us -> 13.4 us  [call(): pl.pallas_call(kernel, out_shape=outs, in_specs=spaces if spaces else [vm...]
  transfers between devices with their start and end apart: 6 -> 6, of which waited for: 2 -> 3; matrix products, arithmetic and copies ran while one was open for 2% -> 2% of each run, Pallas kernels for 12% -> 12%
where the time goes in v1:
time: 37.2 us; the launch traced here: 37 us
  Pallas kernels  13.4 us (36%)
  waiting for transfers between devices  11.3 us (30%)
  starting transfers between devices  10.9 us (29%)
  between operations  0.78 us (2%)
  local copies, waits for them, and re-layouts  0.64 us (2%)
    pallas_call x6, Pallas kernels, call(): pl.pallas_call(kernel, out_shape=outs, in_specs=spaces if spaces else [vm...  13.4 us
    ppermute x1, waiting for transfers between devices, shards(): lax.ppermute(v, 'section', swap)  4.97 us
    ppermute x1, waiting for transfers between devices, shards(): far_y = lax.ppermute(half_y, 'lat', swap_pairs(lats, True, False))  4.96 us
    ppermute x1, starting transfers between devices, shards(): far_y = lax.ppermute(half_y, 'lat', swap_pairs(lats, True, False))  3.05 us
    ppermute x1, starting transfers between devices, shards(): recv_y = lax.ppermute(strip_y, 'lon', swap_pairs(lons, True, True))  2.19 us
    ppermute x1, starting transfers between devices, shards(): recv_x = lax.ppermute(strip_x, 'lon', swap_pairs(lons, False, True))  2.18 us
    ppermute x1, starting transfers between devices, shards(): far_x = lax.ppermute(half_x, 'lat', swap_pairs(lats, False, False))  1.89 us
    ppermute x1, waiting for transfers between devices, shards(): recv_y = lax.ppermute(strip_y, 'lon', swap_pairs(lons, True, True))  1.4 us
  transfers between devices with their start and end apart: 6, of which 3 were waited for; matrix products, arithmetic and copies ran while one was open for 2% of the time, Pallas kernels for 12%

profile of v1, /device:TPU:1, one launch (start us, length us, event | category | flops | bytes accessed | tf_op | source)
XLA Modules:
  0.0 37.0 jit_solution(9117049515827642809)
XLA Ops:
  0.0 0.0 copy-start.6
  0.0 1.6 %shard_map.91.refs_0_ = bf16[2,96,2048]{2,1,0:T(8,128)(2,1)S(1)} custom-call(bf16[2,96,16,128]{3,2,1,0:T(8,128)(2,1)} %fields.1), custom_call_target="tpu_custom_call" | custom-call | tf_op jit(solution)/shard_map/pallas_call | solution.py:263
  1.6 0.0 copy-done.6
  1.7 0.0 copy-start.3
  1.7 0.0 copy-start.4
  1.7 0.6 %shard_map.92 = (bf16[2,64,2048]{2,1,0:T(8,128)(2,1)S(1)}, bf16[2,64,128]{2,1,0:T(8,128)(2,1)S(1)}, bf16[2,64,128]{2,1,0:T(8,128)(2,1)S(1)}) custom-call(bf16[2,96,2048]{2,1,0:T(8,128)(2,1)S(1)} %shard_map.91.refs_0_, bf16[64,96]{1,0:T(8,128)(2,1)S(1)} %copy-done.6), custom_call_target="tpu_custom_call" | custom-call | tf_op jit(solution)/shard_map/pallas_call | solution.py:263
  2.3 0.0 copy-start.7
  2.3 2.2 %collective-permute-start.1 = (bf16[2,64,128]{2,1,0:T(8,128)(2,1)S(1)}, bf16[2,64,128]{2,1,0:T(8,128)(2,1)S(1)}, u32[]{:S(2)}, u32[]{:S(2)}) collective-permute-start(bf16[2,64,128]{2,1,0:T(8,128)(2,1)S(1)} %get-tuple-element.21), channel_id=1, source_target_pairs={{0,1},{1,0},{2,3},{3,2},{4,5},{5,4},{6,7},{7,6},{8,9},{9,8},{10,11... | collective-permute-start | bytes 98312 | tf_op jit(solution)/shard_map/ppermute | solution.py:302
  4.5 2.2 %collective-permute-start.2 = (bf16[2,64,128]{2,1,0:T(8,128)(2,1)S(1)}, bf16[2,64,128]{2,1,0:T(8,128)(2,1)S(1)}, u32[]{:S(2)}, u32[]{:S(2)}) collective-permute-start(bf16[2,64,128]{2,1,0:T(8,128)(2,1)S(1)} %get-tuple-element.22), channel_id=1, source_target_pairs={{1,2},{2,1},{3,0},{0,3},{5,6},{6,5},{7,4},{4,7},{9,10},{10,9},{11,... | collective-permute-start | bytes 98312 | tf_op jit(solution)/shard_map/ppermute | solution.py:301
  6.7 0.0 copy-done.7
  6.7 0.6 %slice.3 = s32[1]{0:T(128)} slice(s32[4]{0:T(128)S(1)} %copy-done.7), slice={[1:2]} | slice | bytes 8 | tf_op jit(solution)/shard_map/slice | solution.py:304
  7.9 0.0 collective-permute-done.1.refs_2_
  8.0 1.4 %collective-permute-done.2.refs_3_ = bf16[2,64,128]{2,1,0:T(8,128)(2,1)S(1)} collective-permute-done((bf16[2,64,128]{2,1,0:T(8,128)(2,1)S(1)}, bf16[2,64,128]{2,1,0:T(8,128)(2,1)S(1)}, u32[]{:S(2)}, u32[]{:S(2)}) %collective-permute-start.2) | collective-permute-done | bytes 32800 | tf_op jit(solution)/shard_map/ppermute | solution.py:301
  9.4 0.0 copy-start
  9.4 0.0 copy-start.1
  9.4 0.0 copy-start.2
  9.4 0.4 %shard_map.93 = (bf16[2,64,1152]{2,1,0:T(8,128)(2,1)S(1)}, bf16[2,64,1152]{2,1,0:T(8,128)(2,1)S(1)}) custom-call(s32[4]{0:T(128)S(1)} %copy-done.7, bf16[2,64,2048]{2,1,0:T(8,128)(2,1)S(1)} %get-tuple-element.20.refs_1_, bf16[2,64,128]{2,1,0:T(8,128)(2,1)S(1)} %collective-permute-done.1.refs_2_, bf16[2,64,128]{2,1,0:T(8,128)(2,1)S(1)} %collective-permute-done.2.refs_3_), custom_call_target="tpu_custom_call" | custom-call | tf_op jit(solution)/shard_map/pallas_call | solution.py:263
  9.8 1.9 %collective-permute-start.3 = (bf16[2,64,1152]{2,1,0:T(8,128)(2,1)S(1)}, bf16[2,64,1152]{2,1,0:T(8,128)(2,1)S(1)}, u32[]{:S(2)}, u32[]{:S(2)}) collective-permute-start(bf16[2,64,1152]{2,1,0:T(8,128)(2,1)S(1)} %get-tuple-element.25.refs_0_), channel_id=1, source_target_pairs={{0,4},{4,0},{8,12},{12,8},{1,5},{5,1},{9,13},{13,9},{2,6},{6,2},{1... | collective-permute-start | bytes 884744 | tf_op jit(solution)/shard_map/ppermute | solution.py:310
  11.7 3.0 %collective-permute-start.4 = (bf16[2,64,1152]{2,1,0:T(8,128)(2,1)S(1)}, bf16[2,64,1152]{2,1,0:T(8,128)(2,1)S(1)}, u32[]{:S(2)}, u32[]{:S(2)}) collective-permute-start(bf16[2,64,1152]{2,1,0:T(8,128)(2,1)S(1)} %get-tuple-element.26.refs_1_), channel_id=1, source_target_pairs={{4,8},{8,4},{5,9},{9,5},{6,10},{10,6},{7,11},{11,7},{20,24},{24,20... | collective-permute-start | bytes 884744 | tf_op jit(solution)/shard_map/ppermute | solution.py:309
  14.7 0.0 collective-permute-done.3.refs_2_
  14.7 5.0 %collective-permute-done.4.refs_3_ = bf16[2,64,1152]{2,1,0:T(8,128)(2,1)S(1)} collective-permute-done((bf16[2,64,1152]{2,1,0:T(8,128)(2,1)S(1)}, bf16[2,64,1152]{2,1,0:T(8,128)(2,1)S(1)}, u32[]{:S(2)}, u32[]{:S(2)}) %collective-permute-start.4) | collective-permute-done | bytes 294944 | tf_op jit(solution)/shard_map/ppermute | solution.py:309
  19.7 0.0 copy-done.3
  19.7 0.0 copy-done.4
  19.7 0.0 copy-done
  19.7 0.0 copy-done.1
  19.7 0.0 copy-done.2
  19.7 0.0 copy-start.5
  19.7 4.6 %shard_map.94 = bf16[64,2048]{1,0:T(8,128)(2,1)S(1)} custom-call(bf16[2,64,1152]{2,1,0:T(8,128)(2,1)S(1)} %get-tuple-element.25.refs_0_, bf16[2,64,1152]{2,1,0:T(8,128)(2,1)S(1)} %get-tuple-element.26.refs_1_, bf16[2,64,1152]{2,1,0:T(8,128)(2,1)S(1)} %collective-permute-done.3.refs_2_, bf16[2,64,1152]{2,1,0:T(8,128)(2,1)S(1)} %collective-permute-done.4.refs_3_, ...), custom_call_target="tpu_custom_call" | custom-call | tf_op jit(solution)/shard_map/pallas_call | solution.py:263
  24.4 1.3 %collective-permute-start.5 = (bf16[64,2048]{1,0:T(8,128)(2,1)S(1)}, bf16[64,2048]{1,0:T(8,128)(2,1)S(1)}, u32[]{:S(2)}, u32[]{:S(2)}) collective-permute-start(bf16[64,2048]{1,0:T(8,128)(2,1)S(1)} %shard_map.94), channel_id=1, source_target_pairs={{0,16},{16,0},{1,17},{17,1},{2,18},{18,2},{3,19},{19,3},{4,20},{20... | collective-permute-start | bytes 786440 | tf_op jit(solution)/shard_map/ppermute | solution.py:332
  25.6 0.0 copy-done.5
  25.6 4.6 %shard_map.95 = (bf16[64,2048]{1,0:T(8,128)(2,1)S(1)}, bf16[64,96]{1,0:T(8,128)(2,1)S(1)}) custom-call(bf16[2,64,1152]{2,1,0:T(8,128)(2,1)S(1)} %get-tuple-element.25.refs_0_, bf16[2,64,1152]{2,1,0:T(8,128)(2,1)S(1)} %get-tuple-element.26.refs_1_, bf16[2,64,1152]{2,1,0:T(8,128)(2,1)S(1)} %collective-permute-done.3.refs_2_, ...), custom_call_target="tpu_custom_call" | custom-call | tf_op jit(solution)/shard_map/pallas_call | solution.py:263
  30.2 5.3 %conditional.1 = (bf16[64,2048]{1,0:T(8,128)(2,1)S(1)}) conditional(s32[]{:T(128)} %convert_element_type.11, bf16[64,2048]{1,0:T(8,128)(2,1)S(1)} %get-tuple-element.28, bf16[64,2048]{1,0:T(8,128)(2,1)S(1)} %get-tuple-element.28), branch_computations={%region_0.0_spmd, %region_1.0_spmd} | conditional | bytes 1572912 | solution.py:334
  30.2 0.3 collective-permute-start
  30.6 5.0 %collective-permute-done = bf16[64,2048]{1,0:T(8,128)(2,1)S(1)} collective-permute-done((bf16[64,2048]{1,0:T(8,128)(2,1)S(1)}, bf16[64,2048]{1,0:T(8,128)(2,1)S(1)}, u32[]{:S(2)}, u32[]{:S(2)}) %collective-permute-start) | collective-permute-done | bytes 262176 | tf_op jit(solution)/shard_map/cond/branch_1_fun/ppermute | solution.py:335
  35.6 0.0 collective-permute-done.5.map_a
  35.6 1.5 %shard_map.96 = bf16[2,96,16,128]{3,2,1,0:T(8,128)(2,1)} custom-call(bf16[64,2048]{1,0:T(8,128)(2,1)S(1)} %collective-permute-done.5.map_a, bf16[64,2048]{1,0:T(8,128)(2,1)S(1)} %get-tuple-element.30.map_b, bf16[64,96]{1,0:T(8,128)(2,1)S(1)} %get-tuple-element.29.w_out), custom_call_target="tpu_custom_call" | custom-call | tf_op jit(solution)/shard_map/pallas_call | solution.py:263
  (1 shorter events, 0.0 us)
Async XLA Ops:
  0.0 1.6 %copy-start.6 = (bf16[64,96]{1,0:T(8,128)(2,1)S(1)}, bf16[64,96]{1,0:T(8,128)(2,1)}, u32[]{:S(2)}) copy-start(bf16[64,96]{1,0:T(8,128)(2,1)} %refs_1_.1) | copy-start | bytes 36868
  1.7 18.1 %copy-start.3 = (bf16[9,64,128]{2,1,0:T(8,128)(2,1)S(1)}, bf16[9,64,128]{2,1,0:T(8,128)(2,1)}, u32[]{:S(2)}) copy-start(bf16[9,64,128]{2,1,0:T(8,128)(2,1)} %refs_8_.3) | copy-start | bytes 442372
  1.7 18.0 %copy-start.4 = (bf16[64,128]{1,0:T(8,128)(2,1)S(1)}, bf16[64,128]{1,0:T(8,128)(2,1)}, u32[]{:S(2)}) copy-start(bf16[64,128]{1,0:T(8,128)(2,1)} %refs_7_.3) | copy-start | bytes 49156
  2.3 4.4 %copy-start.7 = (s32[4]{0:T(128)S(1)}, s32[4]{0:T(128)}, u32[]{:S(2)}) copy-start(s32[4]{0:T(128)} %refs_0_.1) | copy-start | bytes 52
  2.3 5.6 %collective-permute-start.1 = (bf16[2,64,128]{2,1,0:T(8,128)(2,1)S(1)}, bf16[2,64,128]{2,1,0:T(8,128)(2,1)S(1)}, u32[]{:S(2)}, u32[]{:S(2)}) collective-permute-start(bf16[2,64,128]{2,1,0:T(8,128)(2,1)S(1)} %get-tuple-element.21), channel_id=1, source_target_pairs={{0,1},{1,0},{2,3},{3,2},{4,5},{5,4},{6,7},{7,6},{8,9},{9,8},{10,11... | collective-permute-start | bytes 98312 | tf_op jit(solution)/shard_map/ppermute | solution.py:302
  4.5 4.8 %collective-permute-start.2 = (bf16[2,64,128]{2,1,0:T(8,128)(2,1)S(1)}, bf16[2,64,128]{2,1,0:T(8,128)(2,1)S(1)}, u32[]{:S(2)}, u32[]{:S(2)}) collective-permute-start(bf16[2,64,128]{2,1,0:T(8,128)(2,1)S(1)} %get-tuple-element.22), channel_id=1, source_target_pairs={{1,2},{2,1},{3,0},{0,3},{5,6},{6,5},{7,4},{4,7},{9,10},{10,9},{11,... | collective-permute-start | bytes 98312 | tf_op jit(solution)/shard_map/ppermute | solution.py:301
  9.4 10.4 %copy-start = (bf16[9,128,128]{2,1,0:T(8,128)(2,1)S(1)}, bf16[9,128,128]{2,1,0:T(8,128)(2,1)}, u32[]{:S(2)}) copy-start(bf16[9,128,128]{2,1,0:T(8,128)(2,1)} %refs_6_.3) | copy-start | bytes 884740
  9.4 10.4 %copy-start.1 = (bf16[9,64,64]{2,1,0:T(8,128)(2,1)S(1)}, bf16[9,64,64]{2,1,0:T(8,128)(2,1)}, u32[]{:S(2)}) copy-start(bf16[9,64,64]{2,1,0:T(8,128)(2,1)} %refs_4_.3) | copy-start | bytes 221188
  9.4 10.4 %copy-start.2 = (bf16[9,128,64]{1,2,0:T(8,128)(2,1)S(1)}, bf16[9,128,64]{1,2,0:T(8,128)(2,1)}, u32[]{:S(2)}) copy-start(bf16[9,128,64]{1,2,0:T(8,128)(2,1)} %param.15) | copy-start | bytes 442372
  9.8 4.9 %collective-permute-start.3 = (bf16[2,64,1152]{2,1,0:T(8,128)(2,1)S(1)}, bf16[2,64,1152]{2,1,0:T(8,128)(2,1)S(1)}, u32[]{:S(2)}, u32[]{:S(2)}) collective-permute-start(bf16[2,64,1152]{2,1,0:T(8,128)(2,1)S(1)} %get-tuple-element.25.refs_0_), channel_id=1, source_target_pairs={{0,4},{4,0},{8,12},{12,8},{1,5},{5,1},{9,13},{13,9},{2,6},{6,2},{1... | collective-permute-start | bytes 884744 | tf_op jit(solution)/shard_map/ppermute | solution.py:310
  11.7 8.0 %collective-permute-start.4 = (bf16[2,64,1152]{2,1,0:T(8,128)(2,1)S(1)}, bf16[2,64,1152]{2,1,0:T(8,128)(2,1)S(1)}, u32[]{:S(2)}, u32[]{:S(2)}) collective-permute-start(bf16[2,64,1152]{2,1,0:T(8,128)(2,1)S(1)} %get-tuple-element.26.refs_1_), channel_id=1, source_target_pairs={{4,8},{8,4},{5,9},{9,5},{6,10},{10,6},{7,11},{11,7},{20,24},{24,20... | collective-permute-start | bytes 884744 | tf_op jit(solution)/shard_map/ppermute | solution.py:309
  19.7 5.9 %copy-start.5 = (bf16[96,64]{0,1:T(8,128)(2,1)S(1)}, bf16[96,64]{0,1:T(8,128)(2,1)}, u32[]{:S(2)}) copy-start(bf16[96,64]{0,1:T(8,128)(2,1)} %param.19) | copy-start | bytes 36868
  24.4 11.2 %collective-permute-start.5 = (bf16[64,2048]{1,0:T(8,128)(2,1)S(1)}, bf16[64,2048]{1,0:T(8,128)(2,1)S(1)}, u32[]{:S(2)}, u32[]{:S(2)}) collective-permute-start(bf16[64,2048]{1,0:T(8,128)(2,1)S(1)} %shard_map.94), channel_id=1, source_target_pairs={{0,16},{16,0},{1,17},{17,1},{2,18},{18,2},{3,19},{19,3},{4,20},{20... | collective-permute-start | bytes 786440 | tf_op jit(solution)/shard_map/ppermute | solution.py:332
  30.2 5.3 %collective-permute-start = (bf16[64,2048]{1,0:T(8,128)(2,1)S(1)}, bf16[64,2048]{1,0:T(8,128)(2,1)S(1)}, u32[]{:S(2)}, u32[]{:S(2)}) collective-permute-start(bf16[64,2048]{1,0:T(8,128)(2,1)S(1)} %param.1), channel_id=1, source_target_pairs={{0,16},{16,0},{1,17},{17,1},{2,18},{18,2},{3,19},{19,3},{4,20},{20... | collective-permute-start | bytes 786440 | tf_op jit(solution)/shard_map/cond/branch_1_fun/ppermute | solution.py:335

commit v2 on v1

--- a/solution.py
+++ b/solution.py
@@ -11,10 +11,13 @@
 LIMIT_ROWS = 52.7
 
 
-def gelu(x):
-    inner = x * (0.7978845608028654 + 0.035677408136300125 * (x * x))
-    half = 0.5 * x
-    return half + half * jnp.tanh(inner)
+def gelu_of_double(h):
+    inner = h * (1.5957691216057308 + 0.285419265090401 * (h * h))
+    return h + h * jnp.tanh(inner)
+
+
+def halved(weights):
+    return weights * jnp.asarray(0.5, BF)
 
 
 def dot(a, b):
@@ -61,7 +64,7 @@
     samples = picked.shape[0]
     odd = lax.axis_index("lon") % 2
     for b in range(samples):
-        full = gelu(dot(w_in[...], picked[b])).astype(BF)
+        full = gelu_of_double(dot(halved(w_in[...]), picked[b])).astype(BF)
         stem[b] = full
         left = jnp.concatenate([full[:, i * breadth : i * breadth + HALO] for i in range(height)], axis=1)
         right = jnp.concatenate(
@@ -154,8 +157,8 @@
         zz1[base + 2 * c0 : base + 3 * c0] = shift(row, 1)
     skip = []
     for q in range(2):
-        out = dot(paired(enc), zz1[2 * q * 3 * c0 : (2 * q + 4) * 3 * c0])
-        out = (gelu(out) * full_keep).astype(BF)
+        out = dot(halved(paired(enc)), zz1[2 * q * 3 * c0 : (2 * q + 4) * 3 * c0])
+        out = (gelu_of_double(out) * full_keep).astype(BF)
         skip += [out[:c0], out[c0:]]
 
     blocks = -(-lanes // 256)
@@ -196,14 +199,14 @@
     w_down = jnp.concatenate([down[n] for n in range(down.shape[0])], axis=0)
     deep = []
     for h in range(2):
-        out = across(w_down, zz2[h * 3 * c0 : (h + 3) * 3 * c0])
-        deep.append((gelu(out) * half_keep).astype(BF))
+        out = across(halved(w_down), zz2[h * 3 * c0 : (h + 3) * 3 * c0])
+        deep.append((gelu_of_double(out) * half_keep).astype(BF))
     halves(zz3, deep)
     c1 = deep[0].shape[0]
     lifted = []
     for h in range(2):
-        out = dot(by_row(mid), zz3[h * 3 * c1 : (h + 3) * 3 * c1])
-        middle = (gelu(out) + deep[h].astype(F32)).astype(BF)
+        out = dot(halved(by_row(mid)), zz3[h * 3 * c1 : (h + 3) * 3 * c1])
+        middle = (gelu_of_double(out) + deep[h].astype(F32)).astype(BF)
         lifted.append((dot(w_up[...], middle) * half_keep).astype(BF))
     wide_lane = lax.broadcasted_iota(jnp.int32, (128, 256), 1)
     thin_lane = lax.broadcasted_iota(jnp.int32, (128, 256), 0)
@@ -230,8 +233,8 @@
             zz4[base + c0 : base + 2 * c0] = row[:, at : at + span]
     joined = []
     for q in range(2):
-        out = dot(paired(unite), zz4[2 * q * 6 * c0 : (2 * q + 4) * 6 * c0])
-        out = gelu(out).astype(BF)
+        out = dot(halved(paired(unite)), zz4[2 * q * 6 * c0 : (2 * q + 4) * 6 * c0])
+        out = gelu_of_double(out).astype(BF)
         joined += [out[:c0], out[c0:]]
     rest = quarter - start
     pieces = []

time: 37.2 us -> 31.8 us (0.85)
  waiting for transfers between devices: 11.3 us -> 6.37 us
    ppermute x1 -> x0, waiting for transfers between devices: 4.97 us -> none  [shards(): lax.ppermute(v, 'section', swap)]
  transfers between devices with their start and end apart: 6 -> 5, of which waited for: 3 -> 2; matrix products, arithmetic and copies ran while one was open for 2% -> 2% of each run, Pallas kernels for 12% -> 14%
where the time goes in v2:
time: 31.8 us; the launch traced here: 31.6 us
  Pallas kernels  13.2 us (42%)
  starting transfers between devices  10.6 us (33%)
  waiting for transfers between devices  6.37 us (20%)
  between operations  0.78 us (2%)
  local copies, waits for them, and re-layouts  0.62 us (2%)
    pallas_call x6, Pallas kernels, call(): pl.pallas_call(kernel, out_shape=outs, in_specs=spaces if spaces else [vm...  13.2 us
    ppermute x1, waiting for transfers between devices, shards(): far_y = lax.ppermute(half_y, 'lat', swap_pairs(lats, True, False))  4.96 us
    ppermute x1, starting transfers between devices, shards(): far_y = lax.ppermute(half_y, 'lat', swap_pairs(lats, True, False))  3.05 us
    ppermute x1, starting transfers between devices, shards(): recv_y = lax.ppermute(strip_y, 'lon', swap_pairs(lons, True, True))  2.19 us
    ppermute x1, starting transfers between devices, shards(): recv_x = lax.ppermute(strip_x, 'lon', swap_pairs(lons, False, True))  2.18 us
    ppermute x1, starting transfers between devices, shards(): far_x = lax.ppermute(half_x, 'lat', swap_pairs(lats, False, False))  1.89 us
    ppermute x1, waiting for transfers between devices, shards(): recv_y = lax.ppermute(strip_y, 'lon', swap_pairs(lons, True, True))  1.4 us
    ppermute x1, starting transfers between devices, shards(): map_a = lax.ppermute(unet(0)[0], 'section', swap)  1.27 us
  transfers between devices with their start and end apart: 5, of which 2 were waited for; matrix products, arithmetic and copies ran while one was open for 2% of the time, Pallas kernels for 14%

profile of v2, /device:TPU:1, one launch (start us, length us, event | category | flops | bytes accessed | tf_op | source)
XLA Modules:
  0.0 31.6 jit_solution(14155559641040621578)
XLA Ops:
  0.0 0.0 copy-start.6
  0.0 1.6 %shard_map.91.refs_0_ = bf16[2,96,2048]{2,1,0:T(8,128)(2,1)S(1)} custom-call(bf16[2,96,16,128]{3,2,1,0:T(8,128)(2,1)} %fields.1), custom_call_target="tpu_custom_call" | custom-call | tf_op jit(solution)/shard_map/pallas_call | solution.py:266
  1.6 0.0 copy-done.6
  1.7 0.0 copy-start.3
  1.7 0.0 copy-start.4
  1.7 0.6 %shard_map.92 = (bf16[2,64,2048]{2,1,0:T(8,128)(2,1)S(1)}, bf16[2,64,128]{2,1,0:T(8,128)(2,1)S(1)}, bf16[2,64,128]{2,1,0:T(8,128)(2,1)S(1)}) custom-call(bf16[2,96,2048]{2,1,0:T(8,128)(2,1)S(1)} %shard_map.91.refs_0_, bf16[64,96]{1,0:T(8,128)(2,1)S(1)} %copy-done.6), custom_call_target="tpu_custom_call" | custom-call | tf_op jit(solution)/shard_map/pallas_call | solution.py:266
  2.3 0.0 copy-start.7
  2.3 2.2 %collective-permute-start.1 = (bf16[2,64,128]{2,1,0:T(8,128)(2,1)S(1)}, bf16[2,64,128]{2,1,0:T(8,128)(2,1)S(1)}, u32[]{:S(2)}, u32[]{:S(2)}) collective-permute-start(bf16[2,64,128]{2,1,0:T(8,128)(2,1)S(1)} %get-tuple-element.21), channel_id=1, source_target_pairs={{0,1},{1,0},{2,3},{3,2},{4,5},{5,4},{6,7},{7,6},{8,9},{9,8},{10,11... | collective-permute-start | bytes 98312 | tf_op jit(solution)/shard_map/ppermute | solution.py:305
  4.4 2.2 %collective-permute-start.2 = (bf16[2,64,128]{2,1,0:T(8,128)(2,1)S(1)}, bf16[2,64,128]{2,1,0:T(8,128)(2,1)S(1)}, u32[]{:S(2)}, u32[]{:S(2)}) collective-permute-start(bf16[2,64,128]{2,1,0:T(8,128)(2,1)S(1)} %get-tuple-element.22), channel_id=1, source_target_pairs={{1,2},{2,1},{3,0},{0,3},{5,6},{6,5},{7,4},{4,7},{9,10},{10,9},{11,... | collective-permute-start | bytes 98312 | tf_op jit(solution)/shard_map/ppermute | solution.py:304
  6.6 0.0 copy-done.7
  6.6 0.6 %slice.3 = s32[1]{0:T(128)} slice(s32[4]{0:T(128)S(1)} %copy-done.7), slice={[1:2]} | slice | bytes 8 | tf_op jit(solution)/shard_map/slice | solution.py:307
  7.9 0.0 collective-permute-done.1.refs_2_
  7.9 1.4 %collective-permute-done.2.refs_3_ = bf16[2,64,128]{2,1,0:T(8,128)(2,1)S(1)} collective-permute-done((bf16[2,64,128]{2,1,0:T(8,128)(2,1)S(1)}, bf16[2,64,128]{2,1,0:T(8,128)(2,1)S(1)}, u32[]{:S(2)}, u32[]{:S(2)}) %collective-permute-start.2) | collective-permute-done | bytes 32800 | tf_op jit(solution)/shard_map/ppermute | solution.py:304
  9.3 0.0 copy-start
  9.3 0.0 copy-start.1
  9.3 0.0 copy-start.2
  9.3 0.4 %shard_map.93 = (bf16[2,64,1152]{2,1,0:T(8,128)(2,1)S(1)}, bf16[2,64,1152]{2,1,0:T(8,128)(2,1)S(1)}) custom-call(s32[4]{0:T(128)S(1)} %copy-done.7, bf16[2,64,2048]{2,1,0:T(8,128)(2,1)S(1)} %get-tuple-element.20.refs_1_, bf16[2,64,128]{2,1,0:T(8,128)(2,1)S(1)} %collective-permute-done.1.refs_2_, bf16[2,64,128]{2,1,0:T(8,128)(2,1)S(1)} %collective-permute-done.2.refs_3_), custom_call_target="tpu_custom_call" | custom-call | tf_op jit(solution)/shard_map/pallas_call | solution.py:266
  9.7 1.9 %collective-permute-start.3 = (bf16[2,64,1152]{2,1,0:T(8,128)(2,1)S(1)}, bf16[2,64,1152]{2,1,0:T(8,128)(2,1)S(1)}, u32[]{:S(2)}, u32[]{:S(2)}) collective-permute-start(bf16[2,64,1152]{2,1,0:T(8,128)(2,1)S(1)} %get-tuple-element.25.refs_0_), channel_id=1, source_target_pairs={{0,4},{4,0},{8,12},{12,8},{1,5},{5,1},{9,13},{13,9},{2,6},{6,2},{1... | collective-permute-start | bytes 884744 | tf_op jit(solution)/shard_map/ppermute | solution.py:313
  11.6 3.0 %collective-permute-start.4 = (bf16[2,64,1152]{2,1,0:T(8,128)(2,1)S(1)}, bf16[2,64,1152]{2,1,0:T(8,128)(2,1)S(1)}, u32[]{:S(2)}, u32[]{:S(2)}) collective-permute-start(bf16[2,64,1152]{2,1,0:T(8,128)(2,1)S(1)} %get-tuple-element.26.refs_1_), channel_id=1, source_target_pairs={{4,8},{8,4},{5,9},{9,5},{6,10},{10,6},{7,11},{11,7},{20,24},{24,20... | collective-permute-start | bytes 884744 | tf_op jit(solution)/shard_map/ppermute | solution.py:312
  14.7 0.0 collective-permute-done.3.refs_2_
  14.7 5.0 %collective-permute-done.4.refs_3_ = bf16[2,64,1152]{2,1,0:T(8,128)(2,1)S(1)} collective-permute-done((bf16[2,64,1152]{2,1,0:T(8,128)(2,1)S(1)}, bf16[2,64,1152]{2,1,0:T(8,128)(2,1)S(1)}, u32[]{:S(2)}, u32[]{:S(2)}) %collective-permute-start.4) | collective-permute-done | bytes 294944 | tf_op jit(solution)/shard_map/ppermute | solution.py:312
  19.6 0.0 copy-done.3
  19.6 0.0 copy-done.4
  19.6 0.0 copy-done
  19.7 0.0 copy-done.1
  19.7 0.0 copy-done.2
  19.7 0.0 copy-start.5
  19.7 4.6 %shard_map.94 = bf16[64,2048]{1,0:T(8,128)(2,1)S(1)} custom-call(bf16[2,64,1152]{2,1,0:T(8,128)(2,1)S(1)} %get-tuple-element.25.refs_0_, bf16[2,64,1152]{2,1,0:T(8,128)(2,1)S(1)} %get-tuple-element.26.refs_1_, bf16[2,64,1152]{2,1,0:T(8,128)(2,1)S(1)} %collective-permute-done.3.refs_2_, bf16[2,64,1152]{2,1,0:T(8,128)(2,1)S(1)} %collective-permute-done.4.refs_3_, ...), custom_call_target="tpu_custom_call" | custom-call | tf_op jit(solution)/shard_map/pallas_call | solution.py:266
  24.3 1.3 %collective-permute-start.5 = (bf16[64,2048]{1,0:T(8,128)(2,1)S(1)}, bf16[64,2048]{1,0:T(8,128)(2,1)S(1)}, u32[]{:S(2)}, u32[]{:S(2)}) collective-permute-start(bf16[64,2048]{1,0:T(8,128)(2,1)S(1)} %shard_map.94), channel_id=1, source_target_pairs={{0,16},{16,0},{1,17},{17,1},{2,18},{18,2},{3,19},{19,3},{4,20},{20... | collective-permute-start | bytes 786440 | tf_op jit(solution)/shard_map/ppermute | solution.py:335
  25.5 0.0 copy-done.5
  25.5 4.6 %shard_map.95 = (bf16[64,2048]{1,0:T(8,128)(2,1)S(1)}, bf16[64,96]{1,0:T(8,128)(2,1)S(1)}) custom-call(bf16[2,64,1152]{2,1,0:T(8,128)(2,1)S(1)} %get-tuple-element.25.refs_0_, bf16[2,64,1152]{2,1,0:T(8,128)(2,1)S(1)} %get-tuple-element.26.refs_1_, bf16[2,64,1152]{2,1,0:T(8,128)(2,1)S(1)} %collective-permute-done.3.refs_2_, ...), custom_call_target="tpu_custom_call" | custom-call | tf_op jit(solution)/shard_map/pallas_call | solution.py:266
  30.1 0.0 collective-permute-done.5.map_a
  30.1 1.5 %shard_map.96 = bf16[2,96,16,128]{3,2,1,0:T(8,128)(2,1)} custom-call(bf16[64,2048]{1,0:T(8,128)(2,1)S(1)} %collective-permute-done.5.map_a, bf16[64,2048]{1,0:T(8,128)(2,1)S(1)} %get-tuple-element.30.map_b, bf16[64,96]{1,0:T(8,128)(2,1)S(1)} %get-tuple-element.29.w_out), custom_call_target="tpu_custom_call" | custom-call | tf_op jit(solution)/shard_map/pallas_call | solution.py:266
  (1 shorter events, 0.0 us)
Async XLA Ops:
  0.0 1.6 %copy-start.6 = (bf16[64,96]{1,0:T(8,128)(2,1)S(1)}, bf16[64,96]{1,0:T(8,128)(2,1)}, u32[]{:S(2)}) copy-start(bf16[64,96]{1,0:T(8,128)(2,1)} %refs_1_.1) | copy-start | bytes 36868
  1.7 18.0 %copy-start.3 = (bf16[9,64,128]{2,1,0:T(8,128)(2,1)S(1)}, bf16[9,64,128]{2,1,0:T(8,128)(2,1)}, u32[]{:S(2)}) copy-start(bf16[9,64,128]{2,1,0:T(8,128)(2,1)} %refs_8_.3) | copy-start | bytes 442372
  1.7 18.0 %copy-start.4 = (bf16[64,128]{1,0:T(8,128)(2,1)S(1)}, bf16[64,128]{1,0:T(8,128)(2,1)}, u32[]{:S(2)}) copy-start(bf16[64,128]{1,0:T(8,128)(2,1)} %refs_7_.3) | copy-start | bytes 49156
  2.3 4.4 %copy-start.7 = (s32[4]{0:T(128)S(1)}, s32[4]{0:T(128)}, u32[]{:S(2)}) copy-start(s32[4]{0:T(128)} %refs_0_.1) | copy-start | bytes 52
  2.3 5.6 %collective-permute-start.1 = (bf16[2,64,128]{2,1,0:T(8,128)(2,1)S(1)}, bf16[2,64,128]{2,1,0:T(8,128)(2,1)S(1)}, u32[]{:S(2)}, u32[]{:S(2)}) collective-permute-start(bf16[2,64,128]{2,1,0:T(8,128)(2,1)S(1)} %get-tuple-element.21), channel_id=1, source_target_pairs={{0,1},{1,0},{2,3},{3,2},{4,5},{5,4},{6,7},{7,6},{8,9},{9,8},{10,11... | collective-permute-start | bytes 98312 | tf_op jit(solution)/shard_map/ppermute | solution.py:305
  4.4 4.8 %collective-permute-start.2 = (bf16[2,64,128]{2,1,0:T(8,128)(2,1)S(1)}, bf16[2,64,128]{2,1,0:T(8,128)(2,1)S(1)}, u32[]{:S(2)}, u32[]{:S(2)}) collective-permute-start(bf16[2,64,128]{2,1,0:T(8,128)(2,1)S(1)} %get-tuple-element.22), channel_id=1, source_target_pairs={{1,2},{2,1},{3,0},{0,3},{5,6},{6,5},{7,4},{4,7},{9,10},{10,9},{11,... | collective-permute-start | bytes 98312 | tf_op jit(solution)/shard_map/ppermute | solution.py:304
  9.3 10.4 %copy-start = (bf16[9,128,128]{2,1,0:T(8,128)(2,1)S(1)}, bf16[9,128,128]{2,1,0:T(8,128)(2,1)}, u32[]{:S(2)}) copy-start(bf16[9,128,128]{2,1,0:T(8,128)(2,1)} %refs_6_.3) | copy-start | bytes 884740
  9.3 10.4 %copy-start.1 = (bf16[9,64,64]{2,1,0:T(8,128)(2,1)S(1)}, bf16[9,64,64]{2,1,0:T(8,128)(2,1)}, u32[]{:S(2)}) copy-start(bf16[9,64,64]{2,1,0:T(8,128)(2,1)} %refs_4_.3) | copy-start | bytes 221188
  9.3 10.4 %copy-start.2 = (bf16[9,128,64]{1,2,0:T(8,128)(2,1)S(1)}, bf16[9,128,64]{1,2,0:T(8,128)(2,1)}, u32[]{:S(2)}) copy-start(bf16[9,128,64]{1,2,0:T(8,128)(2,1)} %param.15) | copy-start | bytes 442372
  9.7 4.9 %collective-permute-start.3 = (bf16[2,64,1152]{2,1,0:T(8,128)(2,1)S(1)}, bf16[2,64,1152]{2,1,0:T(8,128)(2,1)S(1)}, u32[]{:S(2)}, u32[]{:S(2)}) collective-permute-start(bf16[2,64,1152]{2,1,0:T(8,128)(2,1)S(1)} %get-tuple-element.25.refs_0_), channel_id=1, source_target_pairs={{0,4},{4,0},{8,12},{12,8},{1,5},{5,1},{9,13},{13,9},{2,6},{6,2},{1... | collective-permute-start | bytes 884744 | tf_op jit(solution)/shard_map/ppermute | solution.py:313
  11.6 8.0 %collective-permute-start.4 = (bf16[2,64,1152]{2,1,0:T(8,128)(2,1)S(1)}, bf16[2,64,1152]{2,1,0:T(8,128)(2,1)S(1)}, u32[]{:S(2)}, u32[]{:S(2)}) collective-permute-start(bf16[2,64,1152]{2,1,0:T(8,128)(2,1)S(1)} %get-tuple-element.26.refs_1_), channel_id=1, source_target_pairs={{4,8},{8,4},{5,9},{9,5},{6,10},{10,6},{7,11},{11,7},{20,24},{24,20... | collective-permute-start | bytes 884744 | tf_op jit(solution)/shard_map/ppermute | solution.py:312
  19.7 5.9 %copy-start.5 = (bf16[96,64]{0,1:T(8,128)(2,1)S(1)}, bf16[96,64]{0,1:T(8,128)(2,1)}, u32[]{:S(2)}) copy-start(bf16[96,64]{0,1:T(8,128)(2,1)} %param.19) | copy-start | bytes 36868
  24.3 5.8 %collective-permute-start.5 = (bf16[64,2048]{1,0:T(8,128)(2,1)S(1)}, bf16[64,2048]{1,0:T(8,128)(2,1)S(1)}, u32[]{:S(2)}, u32[]{:S(2)}) collective-permute-start(bf16[64,2048]{1,0:T(8,128)(2,1)S(1)} %shard_map.94), channel_id=1, source_target_pairs={{0,16},{16,0},{1,17},{17,1},{2,18},{18,2},{3,19},{19,3},{4,20},{20... | collective-permute-start | bytes 786440 | tf_op jit(solution)/shard_map/ppermute | solution.py:335
